TPU v7x, 32 devices: a whole 2x2x4 slice. The times are simulated.
32 devices in a mesh: groups: 2 (over x), ref: 16 (over z, y, core).
Axes of the slice: x: 2, y: 2, z: 4, core: 2. Of those that a mesh axis runs over, the one named last changes fastest.
Arguments:
- long_series: bfloat16 [131072], P(('groups', 'ref')), parts along dimension 0, may hold values from -12 to 12
- queries: bfloat16 [64, 1024], P(('groups', 'ref')), parts along dimension 0, may hold values from -48 to 48
- lengths: int32 [64], P(('groups', 'ref')), parts along dimension 0, may hold values from 512 to 1024, as said below
- groups: int32 [64], P(('groups', 'ref')), parts along dimension 0, may hold values from 0 to 15, as said below
Outputs:
- profile: float32 [64, 1024], P(('groups', 'ref')), parts along dimension 0
There are 2 independent parts, one for each index of `groups`. A program takes and returns all parts, laid end to end along the dimension named above; each array names one. Nothing has to cross between parts.
Inputs may be any that keep to these rules, and one draw needn't show every extreme that they name: `lengths`: multiples of 128. `groups`: region g holds reference blocks g * 1 to (g + 1) * 1 - 1; at most 4 queries name one region, and one region is named by exactly 4.
All inputs are finite; a program needn't handle non-finite values.
Results may differ from a plain program's by a relative error of at most 0.0003.
Values may be sent and summed in bfloat16 or wider, within the bound.
A program may use at most 64 MiB of HBM per device.

v0:
```python
import jax
import jax.numpy as jnp
from jax import lax
from jax.sharding import PartitionSpec as P

M = 256
GDEV = 1


SPREAD_FLOOR = 0.25


def from_behind(block, axis, distance):
    devices = range(lax.axis_size(axis))
    route = [(i - distance, i) for i in devices if i - distance in devices]
    return lax.ppermute(block, axis, route)


def window_stats(series, count):
    total = series.shape[0]
    repeated = jnp.tile(series, (M + 1,))[: M * (total + 1)]
    windows = repeated.reshape(M, total + 1)[:, :count]
    values = windows.astype(jnp.float32)
    centre = jnp.mean(values, axis=0)
    spread = jnp.sqrt(jnp.mean((values - centre[None, :]) ** 2, axis=0) + SPREAD_FLOOR)
    return (windows, centre, spread)


def query_stats(series):
    return window_stats(jnp.concatenate([series, jnp.zeros((M,), jnp.bfloat16)]), series.shape[0])


def best_match(query_set, ref_set, usable):
    query_windows, query_centre, query_spread = query_set
    ref_windows, ref_centre, ref_spread = ref_set
    products = lax.dot_general(
        query_windows, ref_windows, (((0,), (0,)), ((), ())), preferred_element_type=jnp.float32
    )
    correlation = (products - M * query_centre[:, None] * ref_centre[None, :]) / (
        M * query_spread[:, None] * ref_spread[None, :]
    )
    correlation = jnp.where(usable[None, :], correlation, -2.0)
    return jnp.max(correlation, axis=1)


def body(long_series, queries, lengths, groups):
    members = lax.axis_size("ref")
    per_device, series_len = queries.shape
    block_len = long_series.shape[0]
    overall = members * block_len
    leading = long_series[:M]
    trailing = from_behind(leading, "ref", -1)
    extended = jnp.concatenate([long_series, trailing])
    pieces = lax.all_gather(extended, "ref", axis=0, tiled=True)

    def match_query(entry_pair):
        series, region = entry_pair
        query_set = query_stats(series)
        best_so_far = jnp.full((series_len,), -2.0, jnp.float32)
        block_index = region * GDEV + 0
        segment = lax.dynamic_slice_in_dim(pieces, block_index * (block_len + M), block_len + M)
        ref_set = window_stats(segment, block_len)
        usable = block_index * block_len + jnp.arange(block_len, dtype=jnp.int32) <= overall - M
        best_so_far = jnp.maximum(best_so_far, best_match(query_set, ref_set, usable))
        return best_so_far

    best_values = lax.map(match_query, (queries, groups))
    live_points = jnp.arange(series_len, dtype=jnp.int32)[None, :] <= lengths[:, None] - M
    return jnp.where(live_points, 2.0 * (1.0 - best_values), 0.0)


def solution(mesh):
    in_specs = (
        P(("groups", "ref")),
        P(("groups", "ref"), None),
        P(("groups", "ref")),
        P(("groups", "ref")),
    )
    out_specs = P(("groups", "ref"), None)
    return jax.shard_map(body, mesh=mesh, in_specs=in_specs, out_specs=out_specs, check_vma=False)
```

profile of v0, /device:TPU:0, one launch (start us, length us, event | category | flops | bytes accessed | tf_op | source)
XLA Modules:
  0.0 84.7 jit_solution(14503548204815174141)
XLA Ops:
  0.0 0.7 slice.27
  0.7 1.3 %collective-permute-start = (bf16[256]{0:T(256)(128)(2,1)S(1)}, bf16[256]{0:T(256)(128)(2,1)S(1)}, u32[]{:S(2)}, u32[]{:S(2)}) collective-permute-start(bf16[256]{0:T(256)(128)(2,1)S(1)} %slice.27), channel_id=1, source_target_pairs={{1,0},{2,1},{3,2},{4,3},{5,4},{6,5},{7,6},{8,7},{9,8},{10,9},{11,1... | collective-permute-start | bytes 1544 | tf_op jit(solution)/shard_map/ppermute | solution.py:16
  2.0 1.2 %broadcast_add_fusion = s32[2]{0:T(128)} fusion(s32[2]{0:T(128)} %param.8), kind=kLoop, calls=%fused_computation.20 | loop fusion | flops 2 | bytes 16 | tf_op jit(solution)/shard_map/sub | solution.py:68
  3.2 0.6 collective-permute-done
  3.7 0.7 pad_maximum_fusion
  4.4 24.0 %all-gather = bf16[16,1,4352]{2,1,0:T(2,128)(2,1)S(1)} all-gather(bf16[1,1,4352]{2,1,0:T(2,128)(2,1)S(1)} %reshape.64), channel_id=1, replica_groups=mesh['groups'=2,'ref'=16] {'ref'}, dimensions={0}, use_global_device_ids=true | all-gather | bytes 147968 | tf_op jit(solution)/shard_map/all_gather | solution.py:54
  28.5 0.8 reduce.1
  29.3 0.2 reshape.65
  29.5 0.0 copy-start.1
  29.5 54.5 %while.13 = (s32[]{:T(128)}, f32[2,1024]{1,0:T(2,128)S(1)}, s32[2]{0:T(128)}, bf16[2,1024]{1,0:T(2,128)(2,1)}, bf16[69632]{0:T(1024)(128)(2,1)S(1)}, /*index=5*/s32[1]{0:T(128)}, s32[1]{0:T(128)}) while((s32[]{:T(128)}, f32[2,1024]{1,0:T(2,128)S(1)}, s32[2]{0:T(128)}, bf16[2,1024]{1,0:T(2,128)(2,1)}, ...), condition=%wide.region_6.7_spmd.clone, body=%wide.region_0.6_spmd.sunk.clone | while | flops 2180528128 | bytes 28354240 | solution.py:67
  29.5 1.3 %dynamic_slice.28 = s32[1]{0:T(128)} dynamic-slice(s32[2]{0:T(128)} %get-tuple-element.149, s32[]{:T(128)} %get-tuple-element.140), dynamic_slice_sizes={1} | dynamic-slice | bytes 12 | tf_op jit(solution)/shard_map/while/body/jit(dynamic_index_in_dim)/dynamic_slice | solution.py:67
  31.4 0.1 dynamic_slice.29
  31.5 0.2 tile.38
  31.6 4.1 %tile.39 = bf16[1118464]{0:T(1024)(128)(2,1)} reshape(bf16[257,4352]{1,0:T(8,128)(2,1)S(1)} %tile.38) | data formatting | bytes 4473856 | tf_op jit(solution)/shard_map/while/body/eval_jaxpr/tile | solution.py:21
  35.7 2.7 %slice.62 = bf16[1114368]{0:T(1024)(128)(2,1)} slice(bf16[1118464]{0:T(1024)(128)(2,1)} %tile.39), slice={[0:1114368]} | slice | bytes 4457472 | tf_op jit(solution)/shard_map/while/body/eval_jaxpr/slice | solution.py:21
  38.4 5.4 %reshape.72 = bf16[256,4353]{1,0:T(8,128)(2,1)S(1)} reshape(bf16[1114368]{0:T(1024)(128)(2,1)} %slice.62) | data formatting | bytes 4457472 | tf_op jit(solution)/shard_map/while/body/eval_jaxpr/reshape | solution.py:22
  43.8 0.0 copy-start
  43.8 0.3 convert_reduce_fusion.6
  44.1 0.6 fusion.16
  44.7 0.0 copy-done
  44.8 1.6 %tile.41 = bf16[328960]{0:T(1024)(128)(2,1)} reshape(bf16[257,1280]{1,0:T(8,128)(2,1)S(1)} %tile.40) | data formatting | bytes 1315840 | tf_op jit(solution)/shard_map/while/body/eval_jaxpr/tile | solution.py:21
  46.4 2.0 %slice.63 = bf16[327936]{0:T(1024)(128)(2,1)} slice(bf16[328960]{0:T(1024)(128)(2,1)} %tile.41), slice={[0:327936]} | slice | bytes 1311744 | tf_op jit(solution)/shard_map/while/body/eval_jaxpr/slice | solution.py:21
  48.4 2.3 %reshape.73 = bf16[256,1281]{1,0:T(8,128)(2,1)S(1)} reshape(bf16[327936]{0:T(1024)(128)(2,1)} %slice.63) | data formatting | bytes 1311744 | tf_op jit(solution)/shard_map/while/body/eval_jaxpr/reshape | solution.py:22
  50.8 0.1 convert_reduce_fusion.7
  50.9 0.2 fusion.17
  51.7 4.9 %select_reduce_fusion.3 = f32[1024]{0:T(1024)S(1)} fusion(f32[4096]{0:T(1024)S(1)} %add_sqrt_fusion.3, f32[1024]{0:T(1024)S(1)} %sqrt_multiply_fusion.3, f32[4096]{0:T(1024)S(1)} %broadcast_multiply_fusion.6, f32[1024]{0:T(1024)S(1)} %convert_reduce_fusion.7, pred[4096]{0:T(1024)(128)(4,1)S(1)} %add_compare_fusion.3, ...), kind=kOutput, calls=%fused_computation.clone.1.clone | convolution fusion | flops 2172648448 | bytes 2670592 | tf_op jit(solution)/shard_map/while/body/eval_jaxpr/dot_general | solution.py:36
  56.7 0.1 dynamic_update_slice.9
  56.7 1.3 %dynamic_slice.28 = s32[1]{0:T(128)} dynamic-slice(s32[2]{0:T(128)} %get-tuple-element.149, s32[]{:T(128)} %get-tuple-element.140), dynamic_slice_sizes={1} | dynamic-slice | bytes 12 | tf_op jit(solution)/shard_map/while/body/jit(dynamic_index_in_dim)/dynamic_slice | solution.py:67
  58.6 0.1 dynamic_slice.29
  58.7 0.2 tile.38
  58.9 4.1 %tile.39 = bf16[1118464]{0:T(1024)(128)(2,1)} reshape(bf16[257,4352]{1,0:T(8,128)(2,1)S(1)} %tile.38) | data formatting | bytes 4473856 | tf_op jit(solution)/shard_map/while/body/eval_jaxpr/tile | solution.py:21
  63.0 2.7 %slice.62 = bf16[1114368]{0:T(1024)(128)(2,1)} slice(bf16[1118464]{0:T(1024)(128)(2,1)} %tile.39), slice={[0:1114368]} | slice | bytes 4457472 | tf_op jit(solution)/shard_map/while/body/eval_jaxpr/slice | solution.py:21
  65.7 5.4 %reshape.72 = bf16[256,4353]{1,0:T(8,128)(2,1)S(1)} reshape(bf16[1114368]{0:T(1024)(128)(2,1)} %slice.62) | data formatting | bytes 4457472 | tf_op jit(solution)/shard_map/while/body/eval_jaxpr/reshape | solution.py:22
  71.0 0.0 copy-start
  71.0 0.3 convert_reduce_fusion.6
  71.4 0.6 fusion.16
  72.0 0.0 copy-done
  72.1 1.6 %tile.41 = bf16[328960]{0:T(1024)(128)(2,1)} reshape(bf16[257,1280]{1,0:T(8,128)(2,1)S(1)} %tile.40) | data formatting | bytes 1315840 | tf_op jit(solution)/shard_map/while/body/eval_jaxpr/tile | solution.py:21
  73.7 2.0 %slice.63 = bf16[327936]{0:T(1024)(128)(2,1)} slice(bf16[328960]{0:T(1024)(128)(2,1)} %tile.41), slice={[0:327936]} | slice | bytes 1311744 | tf_op jit(solution)/shard_map/while/body/eval_jaxpr/slice | solution.py:21
  75.7 2.3 %reshape.73 = bf16[256,1281]{1,0:T(8,128)(2,1)S(1)} reshape(bf16[327936]{0:T(1024)(128)(2,1)} %slice.63) | data formatting | bytes 1311744 | tf_op jit(solution)/shard_map/while/body/eval_jaxpr/reshape | solution.py:22
  78.0 0.1 convert_reduce_fusion.7
  78.1 0.2 fusion.17
  78.9 4.9 %select_reduce_fusion.3 = f32[1024]{0:T(1024)S(1)} fusion(f32[4096]{0:T(1024)S(1)} %add_sqrt_fusion.3, f32[1024]{0:T(1024)S(1)} %sqrt_multiply_fusion.3, f32[4096]{0:T(1024)S(1)} %broadcast_multiply_fusion.6, f32[1024]{0:T(1024)S(1)} %convert_reduce_fusion.7, pred[4096]{0:T(1024)(128)(4,1)S(1)} %add_compare_fusion.3, ...), kind=kOutput, calls=%fused_computation.clone.1.clone | convolution fusion | flops 2172648448 | bytes 2670592 | tf_op jit(solution)/shard_map/while/body/eval_jaxpr/dot_general | solution.py:36
  83.9 0.1 dynamic_update_slice.9
  84.0 0.0 copy-done.1
  84.0 0.7 compare_select_fusion
  (20 shorter events, 0.3 us)
Async XLA Ops:
  0.7 3.0 %collective-permute-start = (bf16[256]{0:T(256)(128)(2,1)S(1)}, bf16[256]{0:T(256)(128)(2,1)S(1)}, u32[]{:S(2)}, u32[]{:S(2)}) collective-permute-start(bf16[256]{0:T(256)(128)(2,1)S(1)} %slice.27), channel_id=1, source_target_pairs={{1,0},{2,1},{3,2},{4,3},{5,4},{6,5},{7,6},{8,7},{9,8},{10,9},{11,1... | collective-permute-start | bytes 1544 | tf_op jit(solution)/shard_map/ppermute | solution.py:16
  29.5 54.5 %copy-start.1 = (s32[2]{0:T(128)S(1)}, s32[2]{0:T(128)}, u32[]{:S(2)}) copy-start(s32[2]{0:T(128)} %broadcast_add_fusion) | copy-start | bytes 28
  43.8 1.0 %copy-start = (bf16[2,1024]{1,0:T(2,128)(2,1)S(1)}, bf16[2,1024]{1,0:T(2,128)(2,1)}, u32[]{:S(2)}) copy-start(bf16[2,1024]{1,0:T(2,128)(2,1)} %get-tuple-element.150) | copy-start | bytes 12292 | tf_op jit(solution)/shard_map/while
  71.0 1.0 %copy-start = (bf16[2,1024]{1,0:T(2,128)(2,1)S(1)}, bf16[2,1024]{1,0:T(2,128)(2,1)}, u32[]{:S(2)}) copy-start(bf16[2,1024]{1,0:T(2,128)(2,1)} %get-tuple-element.150) | copy-start | bytes 12292 | tf_op jit(solution)/shard_map/while
where the time goes:
time: 85.2 us; the launch traced here: 84.7 us
  local copies, waits for them, and re-layouts  40.3 us (47%)
  blocking collectives  24 us (28%)
  matrix products  9.89 us (12%)
  other arithmetic  5.8 us (7%)
  loops' own time  2.79 us (3%)
  starting transfers between devices  1.28 us (2%)
    all_gather x1, blocking collectives, body(): pieces = lax.all_gather(extended, 'ref', axis=0, tiled=True)  24 us
    reshape x4, local copies, waits for them, and re-layouts, window_stats(): windows = repeated.reshape(M, total + 1)[:, :count]  15.4 us
    another operation x8, local copies, waits for them, and re-layouts, window_stats(): repeated = jnp.tile(series, (M + 1,))[:M * (total + 1)]  11.8 us
    dot_general x2, matrix products, best_match(): lax.dot_general(query_windows, ref_windows, (((0,), (0,)), ((), ())), pre...  9.89 us
    slice x4, local copies, waits for them, and re-layouts, window_stats(): repeated = jnp.tile(series, (M + 1,))[:M * (total + 1)]  9.37 us
    another operation x1, loops' own time, body(): best_values = lax.map(match_query, (queries, groups))  2.79 us
    dynamic_slice x4, local copies, waits for them, and re-layouts, body(): best_values = lax.map(match_query, (queries, groups))  2.57 us
  transfers between devices with their start and end apart: 1, of which 1 were waited for; matrix products, arithmetic and copies ran while one was open for 1% of the time, Pallas kernels for 0%

commit v1 on v0

v1 whole, which is shorter than its diff:
```python
import functools

import jax
import jax.numpy as jnp
from jax import lax
from jax.experimental import pallas as pl
from jax.experimental.pallas import tpu as pltpu
from jax.sharding import PartitionSpec as P

M = 256
LANES = 128
HALVES = M // LANES
SPREAD_FLOOR = 0.25
CHUNK = 4
MASKED = -1e30


def hankel(row, following):
    shape = (LANES, LANES)
    lane = lax.broadcasted_iota(jnp.int32, shape, 1)
    sub = lax.broadcasted_iota(jnp.int32, shape, 0)
    here = pltpu.roll(jnp.broadcast_to(row, shape), 1, 1, stride=1, stride_axis=0)
    there = pltpu.roll(jnp.broadcast_to(following, shape), 1, 1, stride=1, stride_axis=0)
    return jnp.where(lane <= sub, here, there)


def toeplitz(row, following):
    shape = (LANES, LANES)
    lane = lax.broadcasted_iota(jnp.int32, shape, 1)
    sub = lax.broadcasted_iota(jnp.int32, shape, 0)
    here = pltpu.roll(jnp.broadcast_to(row, shape), 0, 1, stride=1, stride_axis=0)
    there = pltpu.roll(jnp.broadcast_to(following, shape), 0, 1, stride=1, stride_axis=0)
    return jnp.where(lane >= sub, here, there)


def next_row(x):
    return pltpu.roll(x, x.shape[0] - 1, 0)


def window_stats(x):
    lane = lax.broadcasted_iota(jnp.int32, x.shape, 1)
    total, square = x, jnp.zeros_like(x)
    count = 1
    while count < M:
        def ahead(v):
            if count == LANES:
                return next_row(v)
            rolled = pltpu.roll(v, LANES - count, 1)
            return jnp.where(lane < LANES - count, rolled, next_row(rolled))

        total_ahead, square_ahead = ahead(total), ahead(square)
        gap = total - total_ahead
        square = square + square_ahead + gap * gap * (0.5 / count)
        total = total + total_ahead
        count *= 2
    return total, 1.0 / jnp.sqrt(square * (1.0 / M) + SPREAD_FLOOR)


def join_kernel(members, groups_ref, lengths_ref, q_ref, series_ref, out_ref,
                left_ref, right_ref, mean_ref, total_ref, scale_ref, acc_ref):
    per_device, series_len = q_ref.shape
    q_rows = series_len // LANES
    all_rows = series_ref.shape[0]
    rows = all_rows // members
    full = (series_len - M) // LANES
    tall = full * LANES + 16
    r_pad = rows + 8
    q_pad = q_rows + 8

    flip = (
        lax.broadcasted_iota(jnp.int32, (LANES, LANES), 0)
        + lax.broadcasted_iota(jnp.int32, (LANES, LANES), 1)
        == LANES - 1
    ).astype(jnp.bfloat16)

    parts = []
    for p in range(per_device):
        g = groups_ref[p]
        own = series_ref[pl.ds(pl.multiple_of(g * rows, rows), rows), :].astype(jnp.float32)
        after = jnp.minimum((g + 1) * rows, all_rows - 16)
        extra = series_ref[pl.ds(pl.multiple_of(after, 16), 16), :].astype(jnp.float32)[:8]
        parts += [own, jnp.where(g == members - 1, 0.0, extra)]
    q_all = q_ref[...].astype(jnp.float32)
    for p in range(per_device):
        pieces = [q_all[p : p + 1, LANES * a : LANES * (a + 1)] for a in range(q_rows)]
        parts += pieces + [jnp.zeros((q_pad - q_rows, LANES), jnp.float32)]
    points = jnp.concatenate(parts, axis=0)
    total, scale = window_stats(points)
    total_ref[...] = total
    scale_ref[...] = scale

    for p in range(per_device):
        r_base = p * r_pad
        q_base = per_device * r_pad + p * q_pad
        q_back = jnp.dot(
            points[q_base : q_base + q_pad].astype(jnp.bfloat16), flip, preferred_element_type=jnp.float32
        )
        for a in range(full + HALVES):
            tile = toeplitz(q_back[a : a + 1], q_back[a + 1 : a + 2]).astype(jnp.bfloat16)
            for h in range(HALVES):
                if 0 <= a - h < full:
                    left_ref[pl.ds((a - h) * LANES, LANES), pl.ds(h * LANES, LANES)] = tile
                elif a - h == full:
                    left_ref[pl.ds(full * LANES, 16), pl.ds(h * LANES, LANES)] = tile[:16]
        for m in range(rows + 1):
            right_ref[m] = hankel(
                points[r_base + m : r_base + m + 1], points[r_base + m + 1 : r_base + m + 2]
            ).astype(jnp.bfloat16)
        mean_ref[...] = jnp.dot(
            left_ref[...], jnp.full((M, LANES), 1.0 / M, jnp.bfloat16), preferred_element_type=jnp.float32
        )

        g = groups_ref[p]

        def chunk(first, last):
            right = jnp.concatenate(
                [
                    jnp.concatenate([right_ref[first + h + n] for n in range(CHUNK)], axis=1)
                    for h in range(HALVES)
                ],
                axis=0,
            )
            products = jnp.dot(left_ref[...], right, preferred_element_type=jnp.float32)
            totals = [total_ref[pl.ds(r_base + first + n, 1), :] for n in range(CHUNK)]
            scales = [scale_ref[pl.ds(r_base + first + n, 1), :] for n in range(CHUNK)]
            if last:
                lane = lax.broadcasted_iota(jnp.int32, (1, LANES), 1)
                start = (g * rows + first) * LANES
                limit = all_rows * LANES - M
                floors = [
                    jnp.where(start + n * LANES + lane <= limit, 0.0, MASKED) for n in range(CHUNK)
                ]
            for t in range(0, tall, 16):
                mean = mean_ref[pl.ds(t, 16), :]
                best = None
                for n in range(CHUNK):
                    piece = products[t : t + 16, n * LANES : (n + 1) * LANES]
                    value = (piece - mean * totals[n]) * scales[n]
                    if last:
                        value = value + floors[n]
                    best = value if best is None else jnp.maximum(best, value)
                if not last:
                    best = jnp.maximum(best, acc_ref[pl.ds(t, 16), :])
                acc_ref[pl.ds(t, 16), :] = best

        chunk(rows - CHUNK, True)

        @pl.loop(0, rows // CHUNK - 1)
        def _(c):
            chunk(c * CHUNK, False)

        lane = lax.broadcasted_iota(jnp.int32, (1, LANES), 1)
        limit = lengths_ref[p] - M
        for a in range(q_rows):
            if a < full:
                block = acc_ref[pl.ds(a * LANES, LANES), :]
                best = jnp.max(block.T, axis=0, keepdims=True)
            elif a == full:
                block = acc_ref[pl.ds(a * LANES, 8), :]
                best = jnp.broadcast_to(jnp.max(block, axis=1, keepdims=True)[:1], (1, LANES))
            if a <= full:
                best = best * scale_ref[pl.ds(q_base + a, 1), :] * (1.0 / M)
                row = jnp.where(a * LANES + lane <= limit, 2.0 * (1.0 - best), 0.0)
            else:
                row = jnp.zeros((1, LANES), jnp.float32)
            out_ref[pl.ds(p, 1), pl.ds(a * LANES, LANES)] = row


def join(members, groups, lengths, queries, series):
    per_device, series_len = queries.shape
    rows = series.shape[0] // members
    tall = (series_len - M) // LANES * LANES + 16
    stat_rows = per_device * (rows + 8 + series_len // LANES + 8)
    vmem = pl.BlockSpec(memory_space=pltpu.VMEM)
    smem = pl.BlockSpec(memory_space=pltpu.SMEM)
    return pl.pallas_call(
        functools.partial(join_kernel, members),
        out_shape=jax.ShapeDtypeStruct((per_device, series_len), jnp.float32),
        in_specs=[smem, smem, vmem, vmem],
        out_specs=vmem,
        scratch_shapes=[
            pltpu.VMEM((tall, M), jnp.bfloat16),
            pltpu.VMEM((rows + 1, LANES, LANES), jnp.bfloat16),
            pltpu.VMEM((tall, LANES), jnp.float32),
            pltpu.VMEM((stat_rows, LANES), jnp.float32),
            pltpu.VMEM((stat_rows, LANES), jnp.float32),
            pltpu.VMEM((tall, LANES), jnp.float32),
        ],
        name="join",
    )(groups, lengths, queries, series)


def body(long_series, queries, lengths, groups):
    members = lax.axis_size("ref")
    block = long_series.reshape(-1, LANES)
    series = lax.all_gather(block, "ref", axis=0, tiled=True)
    return join(members, groups, lengths, queries, series)


def solution(mesh):
    in_specs = (
        P(("groups", "ref")),
        P(("groups", "ref"), None),
        P(("groups", "ref")),
        P(("groups", "ref")),
    )
    out_specs = P(("groups", "ref"), None)
    return jax.shard_map(body, mesh=mesh, in_specs=in_specs, out_specs=out_specs, check_vma=False)
```

time: 85.2 us -> 34.3 us (0.40)
  local copies, waits for them, and re-layouts: 40.3 us -> 0 us
  matrix products: 9.89 us -> 0 us
  Pallas kernels: 0 us -> 9.03 us
  other arithmetic: 5.8 us -> 0 us
  loops' own time: 2.79 us -> 0 us
  starting transfers between devices: 1.28 us -> 0 us
  blocking collectives: 24 us -> 25.1 us
    reshape x4 -> x0, local copies, waits for them, and re-layouts: 15.4 us -> none  [window_stats(): windows = repeated.reshape(M, total + 1)[:, :count]]
    another operation x8 -> x0, local copies, waits for them, and re-layouts: 11.8 us -> none  [window_stats(): repeated = jnp.tile(series, (M + 1,))[:M * (total + 1)]]
    slice x5 -> x0, local copies, waits for them, and re-layouts: 10 us -> none  [the longest x4 9.37 us: window_stats(): repeated = jnp.tile(series, (M + 1,))[:M * (total + 1)]]
    dot_general x2 -> x0, matrix products: 9.89 us -> none  [best_match(): lax.dot_general(query_windows, ref_windows, (((0,), (0,)), ((), ())), pre...]
    pallas_call x0 -> x1, Pallas kernels: none -> 9.03 us  [join(): pl.pallas_call(functools.partial(join_kernel, members), out_shape=jax.Sha...]
    another operation x1 -> x0, loops' own time: 2.79 us -> none  [body(): best_values = lax.map(match_query, (queries, groups))]
    dynamic_slice x6 -> x0, local copies, waits for them, and re-layouts: 2.74 us -> none  [the longest x4 2.57 us: body(): best_values = lax.map(match_query, (queries, groups))]
    reduce_sum x8 -> x0, other arithmetic: 2.34 us -> none  [the longest x4 1.46 us: window_stats(): jnp.mean((values - centre[None, :]) ** 2, axis=0) + SPREAD_FLOOR]
  transfers between devices with their start and end apart: 1 -> 0, of which waited for: 1 -> 0; matrix products, arithmetic and copies ran while one was open for 1% -> 0% of each run, Pallas kernels for 0% -> 0%
where the time goes in v1:
time: 34.3 us; the launch traced here: 34.1 us
  blocking collectives  25.1 us (73%)
  Pallas kernels  9.03 us (26%)
    all_gather x1, blocking collectives, body(): series = lax.all_gather(block, 'ref', axis=0, tiled=True)  25.1 us
    pallas_call x1, Pallas kernels, join(): pl.pallas_call(functools.partial(join_kernel, members), out_shape=jax.Sha...  9.03 us

profile of v1, /device:TPU:0, one launch (start us, length us, event | category | flops | bytes accessed | tf_op | source)
XLA Modules:
  0.0 34.1 jit_solution(14047524931147194254)
XLA Ops:
  0.0 25.1 %all_gather.3.series_ref = bf16[512,128]{1,0:T(8,128)(2,1)} all-gather(bf16[32,128]{1,0:T(8,128)(2,1)} %bitcast.1), channel_id=1, replica_groups=mesh['groups'=2,'ref'=16] {'ref'}, dimensions={0}, use_global_device_ids=true | all-gather | bytes 139264 | tf_op jit(solution)/shard_map/all_gather | solution.py:196
  25.1 9.0 %join.1 = f32[2,1024]{1,0:T(2,128)} custom-call(s32[2]{0:T(128)} %groups_ref.1, s32[2]{0:T(128)} %lengths_ref.1, bf16[2,1024]{1,0:T(2,128)(2,1)} %q_ref.1, bf16[512,128]{1,0:T(8,128)(2,1)} %all_gather.3.series_ref), custom_call_target="tpu_custom_call" | custom-call | tf_op jit(solution)/shard_map/join/pallas_call | solution.py:176

commit v2 on v1

--- a/solution.py
+++ b/solution.py
@@ -56,59 +56,111 @@
     return total, 1.0 / jnp.sqrt(square * (1.0 / M) + SPREAD_FLOOR)
 
 
-def join_kernel(members, groups_ref, lengths_ref, q_ref, series_ref, out_ref,
-                left_ref, right_ref, mean_ref, total_ref, scale_ref, acc_ref):
+def to_peers(members, block_ref, series_ref, send_sem, recv_sem, arriving):
+    rows = block_ref.shape[0]
+    me = lax.axis_index("ref")
+
+    def copy(d):
+        owner = lax.rem(me + members - d, members) if arriving else me
+        return pltpu.make_async_remote_copy(
+            src_ref=block_ref,
+            dst_ref=series_ref.at[pl.ds(pl.multiple_of(owner * rows, rows), rows), :],
+            send_sem=send_sem.at[d],
+            recv_sem=recv_sem.at[d],
+            device_id={"ref": lax.rem(me + d, members)},
+            device_id_type=pl.DeviceIdType.MESH,
+        )
+
+    return copy
+
+
+def join_kernel(members, groups_ref, lengths_ref, q_ref, block_ref, out_ref,
+                series_ref, left_ref, right_ref, mean_ref, total_ref, scale_ref, q_scale_ref, acc_ref,
+                send_sem, recv_sem):
     per_device, series_len = q_ref.shape
     q_rows = series_len // LANES
+    rows = block_ref.shape[0]
     all_rows = series_ref.shape[0]
-    rows = all_rows // members
     full = (series_len - M) // LANES
     tall = full * LANES + 16
     r_pad = rows + 8
     q_pad = q_rows + 8
+    me = lax.axis_index("ref")
+
+    barrier = pltpu.get_barrier_semaphore()
+
+    @pl.loop(1, members)
+    def _(d):
+        pl.semaphore_signal(
+            barrier, inc=1, device_id={"ref": lax.rem(me + d, members)}, device_id_type=pl.DeviceIdType.MESH
+        )
+
+    series_ref[pl.ds(pl.multiple_of(me * rows, rows), rows), :] = block_ref[...]
 
     flip = (
         lax.broadcasted_iota(jnp.int32, (LANES, LANES), 0)
         + lax.broadcasted_iota(jnp.int32, (LANES, LANES), 1)
         == LANES - 1
     ).astype(jnp.bfloat16)
-
+    q_all = q_ref[...].astype(jnp.float32)
     parts = []
-    for p in range(per_device):
-        g = groups_ref[p]
-        own = series_ref[pl.ds(pl.multiple_of(g * rows, rows), rows), :].astype(jnp.float32)
-        after = jnp.minimum((g + 1) * rows, all_rows - 16)
-        extra = series_ref[pl.ds(pl.multiple_of(after, 16), 16), :].astype(jnp.float32)[:8]
-        parts += [own, jnp.where(g == members - 1, 0.0, extra)]
-    q_all = q_ref[...].astype(jnp.float32)
     for p in range(per_device):
         pieces = [q_all[p : p + 1, LANES * a : LANES * (a + 1)] for a in range(q_rows)]
         parts += pieces + [jnp.zeros((q_pad - q_rows, LANES), jnp.float32)]
-    points = jnp.concatenate(parts, axis=0)
+    q_points = jnp.concatenate(parts, axis=0)
+    q_scale_ref[...] = window_stats(q_points)[1]
+    q_back = jnp.dot(q_points.astype(jnp.bfloat16), flip, preferred_element_type=jnp.float32)
+    for p in range(per_device):
+        q_base = p * q_pad
+        for a in range(full + HALVES):
+            tile = toeplitz(
+                q_back[q_base + a : q_base + a + 1], q_back[q_base + a + 1 : q_base + a + 2]
+            ).astype(jnp.bfloat16)
+            for h in range(HALVES):
+                if 0 <= a - h < full:
+                    left_ref[p, pl.ds((a - h) * LANES, LANES), pl.ds(h * LANES, LANES)] = tile
+                elif a - h == full:
+                    left_ref[p, pl.ds(full * LANES, 16), pl.ds(h * LANES, LANES)] = tile[:16]
+        mean_ref[p] = jnp.dot(
+            left_ref[p], jnp.full((M, LANES), 1.0 / M, jnp.bfloat16), preferred_element_type=jnp.float32
+        )
+
+    pl.semaphore_wait(barrier, members - 1)
+    outgoing = to_peers(members, block_ref, series_ref, send_sem, recv_sem, False)
+    incoming = to_peers(members, block_ref, series_ref, send_sem, recv_sem, True)
+
+    @pl.loop(1, members)
+    def _(d):
+        outgoing(d).start()
+
+    @pl.loop(1, members)
+    def _(d):
+        incoming(d).wait_recv()
+
+    @pl.loop(1, members)
+    def _(d):
+        outgoing(d).wait_send()
+
+    column = lax.broadcasted_iota(jnp.int32, (r_pad, all_rows), 1)
+    wanted = lax.broadcasted_iota(jnp.int32, (r_pad, all_rows), 0)
+    picks = [
+        jnp.where(column == wanted + groups_ref[p] * rows, 1.0, 0.0).astype(jnp.bfloat16)
+        for p in range(per_device)
+    ]
+    points = jnp.dot(
+        jnp.concatenate(picks, axis=0), series_ref[...], preferred_element_type=jnp.float32
+    )
     total, scale = window_stats(points)
     total_ref[...] = total
     scale_ref[...] = scale
 
     for p in range(per_device):
         r_base = p * r_pad
-        q_base = per_device * r_pad + p * q_pad
-        q_back = jnp.dot(
-            points[q_base : q_base + q_pad].astype(jnp.bfloat16), flip, preferred_element_type=jnp.float32
-        )
-        for a in range(full + HALVES):
-            tile = toeplitz(q_back[a : a + 1], q_back[a + 1 : a + 2]).astype(jnp.bfloat16)
-            for h in range(HALVES):
-                if 0 <= a - h < full:
-                    left_ref[pl.ds((a - h) * LANES, LANES), pl.ds(h * LANES, LANES)] = tile
-                elif a - h == full:
-                    left_ref[pl.ds(full * LANES, 16), pl.ds(h * LANES, LANES)] = tile[:16]
+        q_base = p * q_pad
         for m in range(rows + 1):
             right_ref[m] = hankel(
                 points[r_base + m : r_base + m + 1], points[r_base + m + 1 : r_base + m + 2]
             ).astype(jnp.bfloat16)
-        mean_ref[...] = jnp.dot(
-            left_ref[...], jnp.full((M, LANES), 1.0 / M, jnp.bfloat16), preferred_element_type=jnp.float32
-        )
 
         g = groups_ref[p]
 
@@ -120,7 +172,7 @@
                 ],
                 axis=0,
             )
-            products = jnp.dot(left_ref[...], right, preferred_element_type=jnp.float32)
+            products = jnp.dot(left_ref[p], right, preferred_element_type=jnp.float32)
             totals = [total_ref[pl.ds(r_base + first + n, 1), :] for n in range(CHUNK)]
             scales = [scale_ref[pl.ds(r_base + first + n, 1), :] for n in range(CHUNK)]
             if last:
@@ -131,7 +183,7 @@
                     jnp.where(start + n * LANES + lane <= limit, 0.0, MASKED) for n in range(CHUNK)
                 ]
             for t in range(0, tall, 16):
-                mean = mean_ref[pl.ds(t, 16), :]
+                mean = mean_ref[p, pl.ds(t, 16), :]
                 best = None
                 for n in range(CHUNK):
                     piece = products[t : t + 16, n * LANES : (n + 1) * LANES]
@@ -159,18 +211,19 @@
                 block = acc_ref[pl.ds(a * LANES, 8), :]
                 best = jnp.broadcast_to(jnp.max(block, axis=1, keepdims=True)[:1], (1, LANES))
             if a <= full:
-                best = best * scale_ref[pl.ds(q_base + a, 1), :] * (1.0 / M)
+                best = best * q_scale_ref[pl.ds(q_base + a, 1), :] * (1.0 / M)
                 row = jnp.where(a * LANES + lane <= limit, 2.0 * (1.0 - best), 0.0)
             else:
                 row = jnp.zeros((1, LANES), jnp.float32)
             out_ref[pl.ds(p, 1), pl.ds(a * LANES, LANES)] = row
 
 
-def join(members, groups, lengths, queries, series):
+def join(members, groups, lengths, queries, block):
     per_device, series_len = queries.shape
-    rows = series.shape[0] // members
+    rows = block.shape[0]
     tall = (series_len - M) // LANES * LANES + 16
-    stat_rows = per_device * (rows + 8 + series_len // LANES + 8)
+    r_rows = per_device * (rows + 8)
+    q_rows = per_device * (series_len // LANES + 8)
     vmem = pl.BlockSpec(memory_space=pltpu.VMEM)
     smem = pl.BlockSpec(memory_space=pltpu.SMEM)
     return pl.pallas_call(
@@ -179,22 +232,25 @@
         in_specs=[smem, smem, vmem, vmem],
         out_specs=vmem,
         scratch_shapes=[
-            pltpu.VMEM((tall, M), jnp.bfloat16),
+            pltpu.VMEM((members * rows, LANES), jnp.bfloat16),
+            pltpu.VMEM((per_device, tall, M), jnp.bfloat16),
             pltpu.VMEM((rows + 1, LANES, LANES), jnp.bfloat16),
+            pltpu.VMEM((per_device, tall, LANES), jnp.float32),
+            pltpu.VMEM((r_rows, LANES), jnp.float32),
+            pltpu.VMEM((r_rows, LANES), jnp.float32),
+            pltpu.VMEM((q_rows, LANES), jnp.float32),
             pltpu.VMEM((tall, LANES), jnp.float32),
-            pltpu.VMEM((stat_rows, LANES), jnp.float32),
-            pltpu.VMEM((stat_rows, LANES), jnp.float32),
-            pltpu.VMEM((tall, LANES), jnp.float32),
+            pltpu.SemaphoreType.DMA((members,)),
+            pltpu.SemaphoreType.DMA((members,)),
         ],
+        compiler_params=pltpu.CompilerParams(collective_id=0, has_side_effects=True),
         name="join",
-    )(groups, lengths, queries, series)
+    )(groups, lengths, queries, block)
 
 
 def body(long_series, queries, lengths, groups):
     members = lax.axis_size("ref")
-    block = long_series.reshape(-1, LANES)
-    series = lax.all_gather(block, "ref", axis=0, tiled=True)
-    return join(members, groups, lengths, queries, series)
+    return join(members, groups, lengths, queries, long_series.reshape(-1, LANES))
 
 
 def solution(mesh):

time: 34.3 us -> 20 us (0.58)
  blocking collectives: 25.1 us -> 0 us
  Pallas kernels: 9.03 us -> 18.4 us
  local copies, waits for them, and re-layouts: 0 us -> 1.3 us
    all_gather x1 -> x0, blocking collectives: 25.1 us -> none  [body(): series = lax.all_gather(block, 'ref', axis=0, tiled=True)]
    pallas_call x1, Pallas kernels: 9.03 us -> 18.4 us  [join(): pl.pallas_call(functools.partial(join_kernel, members), out_shape=jax.Sha...]
    unnamed x0 -> x1, local copies, waits for them, and re-layouts: none -> 1.3 us
where the time goes in v2:
time: 20 us; the launch traced here: 19.7 us
  Pallas kernels  18.4 us (92%)
  local copies, waits for them, and re-layouts  1.3 us (6%)
    pallas_call x1, Pallas kernels, join(): pl.pallas_call(functools.partial(join_kernel, members), out_shape=jax.Sha...  18.4 us
    unnamed x1, local copies, waits for them, and re-layouts  1.3 us

profile of v2, /device:TPU:0, one launch (start us, length us, event | category | flops | bytes accessed | tf_op | source)
XLA Modules:
  0.0 19.7 jit_solution(15215996828281008119)
XLA Ops:
  0.0 18.4 %join.1 = f32[2,1024]{1,0:T(2,128)} custom-call(s32[2]{0:T(128)} %groups_ref.1, s32[2]{0:T(128)} %lengths_ref.1, bf16[2,1024]{1,0:T(2,128)(2,1)} %q_ref.1, bf16[32,128]{1,0:T(8,128)(2,1)} %bitcast.1), custom_call_target="tpu_custom_call" | custom-call | tf_op jit(solution)/shard_map/join/pallas_call | solution.py:229
  18.4 1.3 %copy.6 = f32[2,1024]{1,0:T(2,128)} copy(f32[2,1024]{1,0:T(2,128)} %join.1) | data formatting | bytes 16384

commit v3 on v2

--- a/solution.py
+++ b/solution.py
@@ -13,6 +13,7 @@
 SPREAD_FLOOR = 0.25
 CHUNK = 4
 MASKED = -1e30
+NEAR = 4
 
 
 def hankel(row, following):
@@ -56,46 +57,64 @@
     return total, 1.0 / jnp.sqrt(square * (1.0 / M) + SPREAD_FLOOR)
 
 
-def to_peers(members, block_ref, series_ref, send_sem, recv_sem, arriving):
-    rows = block_ref.shape[0]
-    me = lax.axis_index("ref")
-
-    def copy(d):
-        owner = lax.rem(me + members - d, members) if arriving else me
-        return pltpu.make_async_remote_copy(
-            src_ref=block_ref,
-            dst_ref=series_ref.at[pl.ds(pl.multiple_of(owner * rows, rows), rows), :],
-            send_sem=send_sem.at[d],
-            recv_sem=recv_sem.at[d],
-            device_id={"ref": lax.rem(me + d, members)},
-            device_id_type=pl.DeviceIdType.MESH,
-        )
-
-    return copy
-
-
-def join_kernel(members, groups_ref, lengths_ref, q_ref, block_ref, out_ref,
+def ring_order(count):
+    return sorted(range(1, count), key=lambda d: (min(d, count - d), d))
+
+
+def join_kernel(members, groups_hbm, lengths_hbm, q_hbm, block_hbm, out_ref,
                 series_ref, left_ref, right_ref, mean_ref, total_ref, scale_ref, q_scale_ref, acc_ref,
-                send_sem, recv_sem):
+                q_ref, groups_ref, lengths_ref,
+                local_sem, far_send, far_recv, near_send, near_recv):
     per_device, series_len = q_ref.shape
     q_rows = series_len // LANES
-    rows = block_ref.shape[0]
     all_rows = series_ref.shape[0]
+    rows = all_rows // members
     full = (series_len - M) // LANES
     tall = full * LANES + 16
     r_pad = rows + 8
     q_pad = q_rows + 8
+    near = NEAR if members % NEAR == 0 else 1
+    far = members // near
     me = lax.axis_index("ref")
-
+    high, low = me // near, lax.rem(me, near)
+
+    def far_place(d):
+        return lax.rem(high + d, far) * near + low
+
+    def near_place(e):
+        return high * near + lax.rem(low + e, near)
+
+    def slot(owner):
+        return series_ref.at[pl.ds(pl.multiple_of(owner * rows, rows), rows), :]
+
+    def far_copy(d, owner):
+        return pltpu.make_async_remote_copy(
+            src_ref=slot(me), dst_ref=slot(owner), send_sem=far_send.at[d], recv_sem=far_recv.at[d],
+            device_id={"ref": far_place(d)}, device_id_type=pl.DeviceIdType.MESH,
+        )
+
+    def near_copy(e, d, owner):
+        return pltpu.make_async_remote_copy(
+            src_ref=slot(owner), dst_ref=slot(owner),
+            send_sem=near_send.at[e * far + d], recv_sem=near_recv.at[e * far + d],
+            device_id={"ref": near_place(e)}, device_id_type=pl.DeviceIdType.MESH,
+        )
+
+    fetches = [
+        pltpu.make_async_copy(block_hbm, slot(me), local_sem.at[0]),
+        pltpu.make_async_copy(q_hbm, q_ref, local_sem.at[1]),
+        pltpu.make_async_copy(groups_hbm, groups_ref, local_sem.at[2]),
+        pltpu.make_async_copy(lengths_hbm, lengths_ref, local_sem.at[3]),
+    ]
     barrier = pltpu.get_barrier_semaphore()
-
-    @pl.loop(1, members)
-    def _(d):
+    peers = [far_place(d) for d in reversed(ring_order(far))] + [near_place(e) for e in range(1, near)]
+    for peer in peers:
         pl.semaphore_signal(
-            barrier, inc=1, device_id={"ref": lax.rem(me + d, members)}, device_id_type=pl.DeviceIdType.MESH
-        )
-
-    series_ref[pl.ds(pl.multiple_of(me * rows, rows), rows), :] = block_ref[...]
+            barrier, inc=1, device_id={"ref": peer}, device_id_type=pl.DeviceIdType.MESH
+        )
+    for fetch in fetches:
+        fetch.start()
+    fetches[1].wait()
 
     flip = (
         lax.broadcasted_iota(jnp.int32, (LANES, LANES), 0)
@@ -125,21 +144,23 @@
             left_ref[p], jnp.full((M, LANES), 1.0 / M, jnp.bfloat16), preferred_element_type=jnp.float32
         )
 
-    pl.semaphore_wait(barrier, members - 1)
-    outgoing = to_peers(members, block_ref, series_ref, send_sem, recv_sem, False)
-    incoming = to_peers(members, block_ref, series_ref, send_sem, recv_sem, True)
-
-    @pl.loop(1, members)
-    def _(d):
-        outgoing(d).start()
-
-    @pl.loop(1, members)
-    def _(d):
-        incoming(d).wait_recv()
-
-    @pl.loop(1, members)
-    def _(d):
-        outgoing(d).wait_send()
+    fetches[0].wait()
+    pl.semaphore_wait(barrier, len(peers))
+    for d in reversed(ring_order(far)):
+        far_copy(d, me).start()
+    for e in range(1, near):
+        near_copy(e, 0, me).start()
+    for d in ring_order(far):
+        owner = far_place(far - d)
+        far_copy(d, owner).wait_recv()
+        for e in range(1, near):
+            near_copy(e, d, owner).start()
+    fetches[2].wait()
+    fetches[3].wait()
+    for d in [0] + ring_order(far):
+        for e in range(1, near):
+            owner = lax.rem(high + far - d, far) * near + lax.rem(low + near - e, near)
+            near_copy(e, d, owner).wait_recv()
 
     column = lax.broadcasted_iota(jnp.int32, (r_pad, all_rows), 1)
     wanted = lax.broadcasted_iota(jnp.int32, (r_pad, all_rows), 0)
@@ -217,6 +238,12 @@
                 row = jnp.zeros((1, LANES), jnp.float32)
             out_ref[pl.ds(p, 1), pl.ds(a * LANES, LANES)] = row
 
+    for d in ring_order(far):
+        far_copy(d, me).wait_send()
+    for d in range(far):
+        for e in range(1, near):
+            near_copy(e, d, far_place(far - d)).wait_send()
+
 
 def join(members, groups, lengths, queries, block):
     per_device, series_len = queries.shape
@@ -225,11 +252,10 @@
     r_rows = per_device * (rows + 8)
     q_rows = per_device * (series_len // LANES + 8)
     vmem = pl.BlockSpec(memory_space=pltpu.VMEM)
-    smem = pl.BlockSpec(memory_space=pltpu.SMEM)
     return pl.pallas_call(
         functools.partial(join_kernel, members),
         out_shape=jax.ShapeDtypeStruct((per_device, series_len), jnp.float32),
-        in_specs=[smem, smem, vmem, vmem],
+        in_specs=[pl.BlockSpec(memory_space=pl.ANY)] * 4,
         out_specs=vmem,
         scratch_shapes=[
             pltpu.VMEM((members * rows, LANES), jnp.bfloat16),
@@ -240,8 +266,14 @@
             pltpu.VMEM((r_rows, LANES), jnp.float32),
             pltpu.VMEM((q_rows, LANES), jnp.float32),
             pltpu.VMEM((tall, LANES), jnp.float32),
+            pltpu.VMEM((per_device, series_len), jnp.bfloat16),
+            pltpu.SMEM((per_device,), jnp.int32),
+            pltpu.SMEM((per_device,), jnp.int32),
+            pltpu.SemaphoreType.DMA((4,)),
             pltpu.SemaphoreType.DMA((members,)),
             pltpu.SemaphoreType.DMA((members,)),
+            pltpu.SemaphoreType.DMA((NEAR * members,)),
+            pltpu.SemaphoreType.DMA((NEAR * members,)),
         ],
         compiler_params=pltpu.CompilerParams(collective_id=0, has_side_effects=True),
         name="join",

time: 20 us -> 23 us (1.15)
  Pallas kernels: 18.4 us -> 21.5 us
    pallas_call x1, Pallas kernels: 18.4 us -> 21.5 us  [join(): pl.pallas_call(functools.partial(join_kernel, members), out_shape=jax.Sha...]
where the time goes in v3:
time: 23 us; the launch traced here: 22.8 us
  Pallas kernels  21.5 us (93%)
  local copies, waits for them, and re-layouts  1.3 us (6%)
    pallas_call x1, Pallas kernels, join(): pl.pallas_call(functools.partial(join_kernel, members), out_shape=jax.Sha...  21.5 us
    unnamed x1, local copies, waits for them, and re-layouts  1.3 us

profile of v3, /device:TPU:0, one launch (start us, length us, event | category | flops | bytes accessed | tf_op | source)
XLA Modules:
  0.0 22.8 jit_solution(12090695628039818202)
XLA Ops:
  0.0 21.5 %join.1 = f32[2,1024]{1,0:T(2,128)} custom-call(s32[2]{0:T(128)} %groups_hbm.1, s32[2]{0:T(128)} %lengths_hbm.1, bf16[2,1024]{1,0:T(2,128)(2,1)} %q_hbm.1, bf16[32,128]{1,0:T(8,128)(2,1)} %bitcast.1), custom_call_target="tpu_custom_call" | custom-call | tf_op jit(solution)/shard_map/join/pallas_call | solution.py:255
  21.5 1.3 %copy.6 = f32[2,1024]{1,0:T(2,128)} copy(f32[2,1024]{1,0:T(2,128)} %join.1) | data formatting | bytes 16384

commit v4 on v3

--- a/solution.py
+++ b/solution.py
@@ -13,7 +13,7 @@
 SPREAD_FLOOR = 0.25
 CHUNK = 4
 MASKED = -1e30
-NEAR = 4
+NEAR = 1
 
 
 def hankel(row, following):

time: 23 us -> 20.7 us (0.900)
  Pallas kernels: 21.5 us -> 19.2 us
    pallas_call x1, Pallas kernels: 21.5 us -> 19.2 us  [join(): pl.pallas_call(functools.partial(join_kernel, members), out_shape=jax.Sha...]
where the time goes in v4:
time: 20.7 us; the launch traced here: 20.5 us
  Pallas kernels  19.2 us (93%)
  local copies, waits for them, and re-layouts  1.3 us (6%)
    pallas_call x1, Pallas kernels, join(): pl.pallas_call(functools.partial(join_kernel, members), out_shape=jax.Sha...  19.2 us
    unnamed x1, local copies, waits for them, and re-layouts  1.3 us

profile of v4, /device:TPU:0, one launch (start us, length us, event | category | flops | bytes accessed | tf_op | source)
XLA Modules:
  0.0 20.5 jit_solution(13176196755499577571)
XLA Ops:
  0.0 19.2 %join.1 = f32[2,1024]{1,0:T(2,128)} custom-call(s32[2]{0:T(128)} %groups_hbm.1, s32[2]{0:T(128)} %lengths_hbm.1, bf16[2,1024]{1,0:T(2,128)(2,1)} %q_hbm.1, bf16[32,128]{1,0:T(8,128)(2,1)} %bitcast.1), custom_call_target="tpu_custom_call" | custom-call | tf_op jit(solution)/shard_map/join/pallas_call | solution.py:255
  19.2 1.3 %copy.6 = f32[2,1024]{1,0:T(2,128)} copy(f32[2,1024]{1,0:T(2,128)} %join.1) | data formatting | bytes 16384

commit v5 on v2

--- a/solution.py
+++ b/solution.py
@@ -15,13 +15,17 @@
 MASKED = -1e30
 
 
-def hankel(row, following):
+def hankel_tiles(rows):
     shape = (LANES, LANES)
     lane = lax.broadcasted_iota(jnp.int32, shape, 1)
     sub = lax.broadcasted_iota(jnp.int32, shape, 0)
-    here = pltpu.roll(jnp.broadcast_to(row, shape), 1, 1, stride=1, stride_axis=0)
-    there = pltpu.roll(jnp.broadcast_to(following, shape), 1, 1, stride=1, stride_axis=0)
-    return jnp.where(lane <= sub, here, there)
+    rolled = [
+        pltpu.roll(jnp.broadcast_to(row, shape), 1, 1, stride=1, stride_axis=0) for row in rows
+    ]
+    return [
+        jnp.where(lane <= sub, here, there).astype(jnp.bfloat16)
+        for here, there in zip(rolled, rolled[1:])
+    ]
 
 
 def toeplitz(row, following):
@@ -56,46 +60,49 @@
     return total, 1.0 / jnp.sqrt(square * (1.0 / M) + SPREAD_FLOOR)
 
 
-def to_peers(members, block_ref, series_ref, send_sem, recv_sem, arriving):
-    rows = block_ref.shape[0]
-    me = lax.axis_index("ref")
-
-    def copy(d):
-        owner = lax.rem(me + members - d, members) if arriving else me
-        return pltpu.make_async_remote_copy(
-            src_ref=block_ref,
-            dst_ref=series_ref.at[pl.ds(pl.multiple_of(owner * rows, rows), rows), :],
-            send_sem=send_sem.at[d],
-            recv_sem=recv_sem.at[d],
-            device_id={"ref": lax.rem(me + d, members)},
-            device_id_type=pl.DeviceIdType.MESH,
-        )
-
-    return copy
-
-
-def join_kernel(members, groups_ref, lengths_ref, q_ref, block_ref, out_ref,
+def join_kernel(members, groups_hbm, lengths_hbm, q_hbm, block_hbm, out_ref,
                 series_ref, left_ref, right_ref, mean_ref, total_ref, scale_ref, q_scale_ref, acc_ref,
-                send_sem, recv_sem):
+                q_ref, groups_ref, lengths_ref,
+                local_sem, send_sem, recv_sem):
     per_device, series_len = q_ref.shape
     q_rows = series_len // LANES
-    rows = block_ref.shape[0]
     all_rows = series_ref.shape[0]
+    rows = all_rows // members
     full = (series_len - M) // LANES
     tall = full * LANES + 16
-    r_pad = rows + 8
+    r_pad = rows + 16
     q_pad = q_rows + 8
     me = lax.axis_index("ref")
 
+    def place(d):
+        return lax.rem(me + d, members)
+
+    def slot(owner):
+        return series_ref.at[pl.ds(pl.multiple_of(owner * rows, rows), rows), :]
+
+    def copy(d, owner):
+        return pltpu.make_async_remote_copy(
+            src_ref=slot(me), dst_ref=slot(owner), send_sem=send_sem.at[d], recv_sem=recv_sem.at[d],
+            device_id={"ref": place(d)}, device_id_type=pl.DeviceIdType.MESH,
+        )
+
+    fetches = [
+        pltpu.make_async_copy(block_hbm, slot(me), local_sem.at[0]),
+        pltpu.make_async_copy(q_hbm, q_ref, local_sem.at[1]),
+        pltpu.make_async_copy(groups_hbm, groups_ref, local_sem.at[2]),
+        pltpu.make_async_copy(lengths_hbm, lengths_ref, local_sem.at[3]),
+    ]
     barrier = pltpu.get_barrier_semaphore()
+    for fetch in fetches:
+        fetch.start()
 
     @pl.loop(1, members)
     def _(d):
         pl.semaphore_signal(
-            barrier, inc=1, device_id={"ref": lax.rem(me + d, members)}, device_id_type=pl.DeviceIdType.MESH
+            barrier, inc=1, device_id={"ref": place(d)}, device_id_type=pl.DeviceIdType.MESH
         )
 
-    series_ref[pl.ds(pl.multiple_of(me * rows, rows), rows), :] = block_ref[...]
+    fetches[1].wait()
 
     flip = (
         lax.broadcasted_iota(jnp.int32, (LANES, LANES), 0)
@@ -125,21 +132,19 @@
             left_ref[p], jnp.full((M, LANES), 1.0 / M, jnp.bfloat16), preferred_element_type=jnp.float32
         )
 
+    fetches[0].wait()
     pl.semaphore_wait(barrier, members - 1)
-    outgoing = to_peers(members, block_ref, series_ref, send_sem, recv_sem, False)
-    incoming = to_peers(members, block_ref, series_ref, send_sem, recv_sem, True)
-
-    @pl.loop(1, members)
-    def _(d):
-        outgoing(d).start()
-
-    @pl.loop(1, members)
-    def _(d):
-        incoming(d).wait_recv()
-
-    @pl.loop(1, members)
-    def _(d):
-        outgoing(d).wait_send()
+
+    @pl.loop(1, members)
+    def _(d):
+        copy(d, me).start()
+
+    fetches[2].wait()
+    fetches[3].wait()
+
+    @pl.loop(1, members)
+    def _(d):
+        copy(d, place(members - d)).wait_recv()
 
     column = lax.broadcasted_iota(jnp.int32, (r_pad, all_rows), 1)
     wanted = lax.broadcasted_iota(jnp.int32, (r_pad, all_rows), 0)
@@ -157,10 +162,9 @@
     for p in range(per_device):
         r_base = p * r_pad
         q_base = p * q_pad
-        for m in range(rows + 1):
-            right_ref[m] = hankel(
-                points[r_base + m : r_base + m + 1], points[r_base + m + 1 : r_base + m + 2]
-            ).astype(jnp.bfloat16)
+        tiles = hankel_tiles([points[r_base + m : r_base + m + 1] for m in range(rows + HALVES)])
+        for m, tile in enumerate(tiles):
+            right_ref[m] = tile
 
         g = groups_ref[p]
 
@@ -217,19 +221,22 @@
                 row = jnp.zeros((1, LANES), jnp.float32)
             out_ref[pl.ds(p, 1), pl.ds(a * LANES, LANES)] = row
 
+    @pl.loop(1, members)
+    def _(d):
+        copy(d, me).wait_send()
+
 
 def join(members, groups, lengths, queries, block):
     per_device, series_len = queries.shape
     rows = block.shape[0]
     tall = (series_len - M) // LANES * LANES + 16
-    r_rows = per_device * (rows + 8)
+    r_rows = per_device * (rows + 16)
     q_rows = per_device * (series_len // LANES + 8)
     vmem = pl.BlockSpec(memory_space=pltpu.VMEM)
-    smem = pl.BlockSpec(memory_space=pltpu.SMEM)
     return pl.pallas_call(
         functools.partial(join_kernel, members),
-        out_shape=jax.ShapeDtypeStruct((per_device, series_len), jnp.float32),
-        in_specs=[smem, smem, vmem, vmem],
+        out_shape=pltpu.VMEM((per_device, series_len), jnp.float32),
+        in_specs=[pl.BlockSpec(memory_space=pl.ANY)] * 4,
         out_specs=vmem,
         scratch_shapes=[
             pltpu.VMEM((members * rows, LANES), jnp.bfloat16),
@@ -240,6 +247,10 @@
             pltpu.VMEM((r_rows, LANES), jnp.float32),
             pltpu.VMEM((q_rows, LANES), jnp.float32),
             pltpu.VMEM((tall, LANES), jnp.float32),
+            pltpu.VMEM((per_device, series_len), jnp.bfloat16),
+            pltpu.SMEM((per_device,), jnp.int32),
+            pltpu.SMEM((per_device,), jnp.int32),
+            pltpu.SemaphoreType.DMA((4,)),
             pltpu.SemaphoreType.DMA((members,)),
             pltpu.SemaphoreType.DMA((members,)),
         ],

time: 20 us -> 18.1 us (0.905)
  Pallas kernels: 18.4 us -> 17.3 us
  local copies, waits for them, and re-layouts: 1.3 us -> 0.6 us
    pallas_call x1, Pallas kernels: 18.4 us -> 17.3 us  [join(): pl.pallas_call(functools.partial(join_kernel, members), out_shape=pltpu.V...]
    unnamed x1, local copies, waits for them, and re-layouts: 1.3 us -> 0.6 us
where the time goes in v5:
time: 18.1 us; the launch traced here: 17.9 us
  Pallas kernels  17.3 us (96%)
  local copies, waits for them, and re-layouts  0.6 us (3%)
    pallas_call x1, Pallas kernels, join(): pl.pallas_call(functools.partial(join_kernel, members), out_shape=pltpu.V...  17.3 us
    unnamed x1, local copies, waits for them, and re-layouts  0.6 us

profile of v5, /device:TPU:0, one launch (start us, length us, event | category | flops | bytes accessed | tf_op | source)
XLA Modules:
  0.0 17.9 jit_solution(9163007843091018587)
XLA Ops:
  0.0 17.3 %join.1 = f32[2,1024]{1,0:T(2,128)S(1)} custom-call(s32[2]{0:T(128)} %groups_hbm.1, s32[2]{0:T(128)} %lengths_hbm.1, bf16[2,1024]{1,0:T(2,128)(2,1)} %q_hbm.1, bf16[32,128]{1,0:T(8,128)(2,1)} %bitcast.1), custom_call_target="tpu_custom_call" | custom-call | tf_op jit(solution)/shard_map/join/pallas_call | solution.py:236
  17.3 0.6 %copy.6 = f32[2,1024]{1,0:T(2,128)} copy(f32[2,1024]{1,0:T(2,128)S(1)} %join.1) | data formatting | bytes 16384

commit v6 on v5

--- a/solution.py
+++ b/solution.py
@@ -61,7 +61,7 @@
 
 
 def join_kernel(members, groups_hbm, lengths_hbm, q_hbm, block_hbm, out_ref,
-                series_ref, left_ref, right_ref, mean_ref, total_ref, scale_ref, q_scale_ref, acc_ref,
+                series_ref, left_ref, right_ref, mean_ref, total_ref, scale_ref, q_scale_ref, acc_ref, even_ref, odd_ref,
                 q_ref, groups_ref, lengths_ref,
                 local_sem, send_sem, recv_sem):
     per_device, series_len = q_ref.shape
@@ -168,7 +168,7 @@
 
         g = groups_ref[p]
 
-        def chunk(first, last):
+        def multiply(products_ref, first):
             right = jnp.concatenate(
                 [
                     jnp.concatenate([right_ref[first + h + n] for n in range(CHUNK)], axis=1)
@@ -176,7 +176,9 @@
                 ],
                 axis=0,
             )
-            products = jnp.dot(left_ref[p], right, preferred_element_type=jnp.float32)
+            products_ref[...] = jnp.dot(left_ref[p], right, preferred_element_type=jnp.float32)
+
+        def fold(products_ref, first, last):
             totals = [total_ref[pl.ds(r_base + first + n, 1), :] for n in range(CHUNK)]
             scales = [scale_ref[pl.ds(r_base + first + n, 1), :] for n in range(CHUNK)]
             if last:
@@ -190,7 +192,7 @@
                 mean = mean_ref[p, pl.ds(t, 16), :]
                 best = None
                 for n in range(CHUNK):
-                    piece = products[t : t + 16, n * LANES : (n + 1) * LANES]
+                    piece = products_ref[pl.ds(t, 16), pl.ds(n * LANES, LANES)]
                     value = (piece - mean * totals[n]) * scales[n]
                     if last:
                         value = value + floors[n]
@@ -199,11 +201,19 @@
                     best = jnp.maximum(best, acc_ref[pl.ds(t, 16), :])
                 acc_ref[pl.ds(t, 16), :] = best
 
-        chunk(rows - CHUNK, True)
-
-        @pl.loop(0, rows // CHUNK - 1)
-        def _(c):
-            chunk(c * CHUNK, False)
+        multiply(even_ref, rows - CHUNK)
+        multiply(odd_ref, 0)
+        fold(even_ref, rows - CHUNK, True)
+
+        @pl.loop(0, rows // (2 * CHUNK) - 1)
+        def _(i):
+            first = 2 * CHUNK * i
+            multiply(even_ref, first + CHUNK)
+            fold(odd_ref, first, False)
+            multiply(odd_ref, first + 2 * CHUNK)
+            fold(even_ref, first + CHUNK, False)
+
+        fold(odd_ref, rows - 2 * CHUNK, False)
 
         lane = lax.broadcasted_iota(jnp.int32, (1, LANES), 1)
         limit = lengths_ref[p] - M
@@ -247,6 +257,8 @@
             pltpu.VMEM((r_rows, LANES), jnp.float32),
             pltpu.VMEM((q_rows, LANES), jnp.float32),
             pltpu.VMEM((tall, LANES), jnp.float32),
+            pltpu.VMEM((tall, CHUNK * LANES), jnp.float32),
+            pltpu.VMEM((tall, CHUNK * LANES), jnp.float32),
             pltpu.VMEM((per_device, series_len), jnp.bfloat16),
             pltpu.SMEM((per_device,), jnp.int32),
             pltpu.SMEM((per_device,), jnp.int32),

time: 18.1 us -> 17 us (0.939)
  Pallas kernels: 17.3 us -> 16.2 us
    pallas_call x1, Pallas kernels: 17.3 us -> 16.2 us  [join(): pl.pallas_call(functools.partial(join_kernel, members), out_shape=pltpu.V...]
where the time goes in v6:
time: 17 us; the launch traced here: 16.9 us
  Pallas kernels  16.2 us (95%)
  local copies, waits for them, and re-layouts  0.6 us (4%)
    pallas_call x1, Pallas kernels, join(): pl.pallas_call(functools.partial(join_kernel, members), out_shape=pltpu.V...  16.2 us
    unnamed x1, local copies, waits for them, and re-layouts  0.6 us

profile of v6, /device:TPU:0, one launch (start us, length us, event | category | flops | bytes accessed | tf_op | source)
XLA Modules:
  0.0 16.9 jit_solution(12539788232753212034)
XLA Ops:
  0.0 16.2 %join.1 = f32[2,1024]{1,0:T(2,128)S(1)} custom-call(s32[2]{0:T(128)} %groups_hbm.1, s32[2]{0:T(128)} %lengths_hbm.1, bf16[2,1024]{1,0:T(2,128)(2,1)} %q_hbm.1, bf16[32,128]{1,0:T(8,128)(2,1)} %bitcast.1), custom_call_target="tpu_custom_call" | custom-call | tf_op jit(solution)/shard_map/join/pallas_call | solution.py:246
  16.3 0.6 %copy.6 = f32[2,1024]{1,0:T(2,128)} copy(f32[2,1024]{1,0:T(2,128)S(1)} %join.1) | data formatting | bytes 16384
